TPU v7x, 512 devices: a whole 4x8x8 slice. The times are simulated.
512 devices in a mesh: dom: 64 (over z_lo, y, core), ch: 8 (over z_hi, x).
Axes of the slice: x: 4, y: 8, z: 8 (z_hi: 2, z_lo: 4; z = z_hi * 4 + z_lo), core: 2. Of those that a mesh axis runs over, the one named last changes fastest.
Arguments:
- node_irreps: bfloat16 [49, 128, 1024], P(None, 'ch', 'dom'), may hold values from -6 to 6
- out_grad: bfloat16 [49, 128, 1024], P(None, 'ch', 'dom'), may hold values from -6 to 6
- edge_source: int32 [8, 1024], P(None, 'dom'), may hold values from 0 to 31
- edge_rotation: int32 [8, 1024], P(None, 'dom'), may hold values from 0 to 255
- edge_count: int32 [1024], P('dom'), may hold values from 1 to 8
- ghost_slot: int32 [1024], P('dom'), may hold values from 0 to 15, as said below
- wigner: float32 [455, 16384], P(None, 'dom'), may hold values from -1 to 1, as said below
- so2_m0: bfloat16 [7, 128, 7, 128], P(None, 'ch'), may hold values from -0.1875 to 0.1875
- so2_m1: bfloat16 [2, 6, 128, 6, 128], P(None, None, 'ch'), may hold values from -0.15625 to 0.15625
- so2_m2: bfloat16 [2, 5, 128, 5, 128], P(None, None, 'ch'), may hold values from -0.15625 to 0.15625
- attn_vector: float32 [128], P('ch'), may hold values from -60 to 60
Outputs:
- updated: bfloat16 [49, 128, 1024], P(None, 'ch', 'dom')
- irreps_grad: float32 [49, 128, 1024], P(None, 'ch', 'dom')
Inputs may be any that keep to these rules, and one draw needn't show every extreme that they name: `edge_source`: slots below 16 are the domain's own atoms in order; slot 16 + g is the domain's ghost g. `edge_rotation`: picks one of the 256 columns of wigner that belong to the atom's domain. Slots j < edge_count[a] are live, the others padding. `ghost_slot`: of a domain's 16 entries, the first 8 name atoms of the previous domain (cyclically) among its last 16 slots, the others atoms of the next domain among its first 16 slots. `wigner`: each column holds for l = 0..6 an orthogonal (2l+1) x (2l+1) block, row-major, blocks in order of l.
All inputs are finite; a program needn't handle non-finite values.
Results may differ from a plain program's by a relative error of at most 0.012.
The roundings to bfloat16 on the way count: a program that leaves them out, or rounds other values in their place, can miss the bound.
Values may be sent and summed in bfloat16 or wider, within the bound.
A program may use at most 128 MiB of HBM per device.

v0:
```python
import jax
import jax.numpy as jnp
from jax import lax
from jax.experimental import pallas as pl
from jax.experimental.pallas import tpu as pltpu
from jax.sharding import PartitionSpec as P

LMAX = 6
MMAX = 2
K = 49
OWN = 16
EDGES = 128
KP = 56
ROWS = 2 * KP
PITCH = 116
F32 = jnp.float32
BF16 = jnp.bfloat16
MESH = pl.DeviceIdType.MESH


def rows_of_levels():
    levels = []
    offset = 0
    for level in range(LMAX + 1):
        width = 2 * level + 1
        reach = min(level, MMAX)
        orders = list(range(-reach, reach + 1))
        levels.append((level, width, offset, orders))
        offset += width * width
    return levels


LEVELS = rows_of_levels()


def place(level, order):
    if order == 0:
        return level
    if order == 1:
        return 6 + level
    if order == -1:
        return 12 + level
    if order == 2:
        return 17 + level
    return 22 + level


def iota(shape, dim):
    return lax.broadcasted_iota(jnp.int32, shape, dim)


def one_where(cond):
    return jnp.where(cond, 1.0, 0.0).astype(BF16)


def spin(x, shift):
    return pltpu.roll(x, shift, 1)


def dot(a, b):
    return jnp.dot(a, b, preferred_element_type=F32)


def turn(wige, level, width, offset, order, col):
    row = offset + (level + order) * width + col
    return jnp.broadcast_to(wige[row : row + 1, :], (8, EDGES))


def rotate_in(mixed, wige, feats, write):
    for c in range(8):
        feats[c * PITCH : c * PITCH + ROWS, :] = mixed[:, c * EDGES : (c + 1) * EDGES]
    for level, width, offset, orders in LEVELS:
        acc = {}
        for col in range(width):
            k = level * level + col
            low = feats[pl.ds(k, 8, stride=PITCH), :]
            high = feats[pl.ds(KP + k, 8, stride=PITCH), :]
            for order in orders:
                w = turn(wige, level, width, offset, order, col)
                if col == 0:
                    acc[order] = (w * low, w * high)
                else:
                    a, b = acc[order]
                    acc[order] = (a + w * low, b + w * high)
        for order in orders:
            write(place(level, order), jnp.concatenate(acc[order], 0))


def rotate_out(read, wige, back):
    for level, width, offset, orders in LEVELS:
        mine = {order: read(place(level, order)) for order in orders}
        for col in range(width):
            k = level * level + col
            low = high = None
            for order in orders:
                w = turn(wige, level, width, offset, order, col)
                a, b = mine[order]
                low = w * a if low is None else low + w * a
                high = w * b if high is None else high + w * b
            back[pl.ds(k, 8, stride=PITCH), :] = low
            back[pl.ds(KP + k, 8, stride=PITCH), :] = high


def across(back):
    return jnp.concatenate([back[c * PITCH : c * PITCH + ROWS, :] for c in range(8)], 1)


def to_rows(ref, pad):
    pad[...] = jnp.zeros_like(pad)
    pad[:, 0:K] = ref[...].astype(F32).reshape(256, K)
    low = pad[0:128, :].T
    high = pad[128:256, :].T
    return jnp.concatenate([low[0:KP], high[0:KP]], 0)


def from_rows(rows):
    fill = jnp.zeros((128 - KP, 128), F32)
    low = jnp.concatenate([rows[0:KP], fill], 0).T
    high = jnp.concatenate([rows[KP:ROWS], fill], 0).T
    return jnp.concatenate([low, high], 0)[:, 0:K].reshape(16, 16, K)


def body(
    x_ref,
    g_ref,
    src_ref,
    turn_ref,
    cnt_ref,
    slot_ref,
    wig_ref,
    w0_ref,
    w1_ref,
    w2_ref,
    attn_ref,
    upd_ref,
    grad_ref,
    tab,
    pad,
    wige,
    gat,
    sca,
    gat_tile,
    sca_tile,
    feats,
    back,
    rot,
    drot,
    ys,
    ps,
    wt0,
    wt1,
    wt2,
    accum,
    below_out,
    above_out,
    from_above,
    from_below,
    x_out,
    x_in,
    z_out,
    z_in,
    red,
    send_sem,
    tab_sem,
    ghost_send,
    ghost_recv,
    xs_send,
    xs_recv,
    zs_send,
    zs_recv,
):
    doms = lax.axis_size("dom")
    d = lax.axis_index("dom")
    ch = lax.axis_index("ch")
    zh = ch // 4
    xi = lax.rem(ch, 4)
    up = (lax.rem(d + 1, doms), ch)
    down = (lax.rem(d + doms - 1, doms), ch)
    other = (d, lax.rem(ch + 4, 8))

    def peer(off):
        return (d, zh * 4 + lax.rem(xi + off, 4))

    barrier = pltpu.get_barrier_semaphore()
    for target in (up, down, other, peer(1), peer(2), peer(3)):
        pl.semaphore_signal(barrier, inc=1, device_id=target, device_id_type=MESH)

    tab[0, ch] = to_rows(x_ref, pad).astype(BF16)

    def rcopy(src, dst, ssem, rsem, target):
        return pltpu.make_async_remote_copy(
            src_ref=src,
            dst_ref=dst,
            send_sem=ssem,
            recv_sem=rsem,
            device_id=target,
            device_id_type=MESH,
        )

    def table_copy(blk, who, n, target):
        return rcopy(
            tab.at[0, who], tab.at[blk, who], send_sem.at[n], tab_sem.at[blk, who], target
        )

    def arrival(blk, who):
        return rcopy(
            tab.at[0, who], tab.at[blk, who], send_sem.at[0], tab_sem.at[blk, who], up
        ).wait_recv()

    pl.semaphore_wait(barrier, 6)
    sends = []

    def go(blk, who, target):
        copy = table_copy(blk, who, len(sends), target)
        copy.start()
        sends.append(copy)

    go(0, ch, other)
    for off in (2, 1, 3):
        go(0, ch, peer(off))
    go(1, ch, up)
    go(2, ch, down)

    spread = one_where(lax.rem(iota((16, EDGES), 1), 16) == iota((16, EDGES), 0))
    pick = (iota((8, EDGES), 1) // 16) == iota((8, EDGES), 0)

    def edge_row(ref):
        wide = dot(ref[...].astype(F32).astype(BF16), spread)
        return jnp.sum(jnp.where(pick, wide, 0.0), axis=0, keepdims=True)

    src = edge_row(src_ref)
    turns = edge_row(turn_ref)
    lane = iota((1, EDGES), 1)
    atom = lax.rem(lane, 16)
    ghost = jnp.zeros((1, EDGES), F32)
    count = jnp.zeros((1, EDGES), jnp.int32)
    for a in range(16):
        ghost = jnp.where(src == 16.0 + a, slot_ref[a].astype(F32), ghost)
        count = jnp.where(atom == a, cnt_ref[a], count)
    nowhere = -1000.0
    index = (
        jnp.where(src < 16.0, src, nowhere),
        jnp.where((src >= 16.0) & (src < 24.0), ghost, nowhere),
        jnp.where(src >= 24.0, ghost, nowhere),
    )
    row_id = iota((EDGES, EDGES), 0).astype(F32)
    lane_id = iota((EDGES, EDGES), 1).astype(F32)
    for blk in range(4):
        idx = atom.astype(F32) if blk == 3 else index[blk]
        wide = jnp.broadcast_to(idx, (EDGES, EDGES))
        tall = wide.T
        for c in range(8):
            forth = one_where(row_id == wide + 16.0 * c)
            fro = one_where(lane_id == tall + 16.0 * c)
            if blk == 3:
                gat_tile[:, c * 128 : c * 128 + 128] = forth
                sca_tile[c * 128 : c * 128 + 128, :] = fro
            else:
                gat[blk * 128 : blk * 128 + 128, c * 128 : c * 128 + 128] = forth
                sca[c * 128 : c * 128 + 128, blk * 128 : blk * 128 + 128] = fro

    chosen = one_where(iota((256, EDGES), 0).astype(F32) == jnp.broadcast_to(turns, (256, EDGES)))
    whole = wig_ref[...]
    first = whole.astype(BF16)
    rest = whole - first.astype(F32)
    second = rest.astype(BF16)
    third = (rest - second.astype(F32)).astype(BF16)
    wige[...] = dot(first, chosen) + (dot(second, chosen) + dot(third, chosen))

    def keep_p(pos, value):
        ps[pos] = value

    rotate_in(dot(to_rows(g_ref, pad).astype(BF16), gat_tile[...]), wige, feats, keep_p)

    for lev in range(7):
        tile = w0_ref[:, lev].reshape(112, 128).astype(F32)
        wt0[lev * 128 : lev * 128 + 128, :] = (
            jnp.concatenate([tile, jnp.zeros((16, 128), F32)], 0).T.astype(BF16)
        )
    for ref, out, n in ((w1_ref, wt1, 6), (w2_ref, wt2, 5)):
        for part in range(2):
            for lev in range(n):
                tile = ref[part, :, lev].reshape(n * 16, 128).astype(F32)
                tile = jnp.concatenate([tile, jnp.zeros((128 - n * 16, 128), F32)], 0)
                out[lev * 128 : lev * 128 + 128, part * 128 : part * 128 + 128] = (
                    tile.T.astype(BF16)
                )
    back[...] = jnp.zeros_like(back)

    near = [zh * 4 + lax.rem(xi + off, 4) for off in (1, 3, 2)]
    far = [(1 - zh) * 4 + lax.rem(xi + off, 4) for off in (1, 3, 2)]
    mirror = lax.rem(ch + 4, 8)
    arrival(0, near[0])
    go(1, near[0], up)
    go(2, near[0], down)
    arrival(0, near[1])
    go(1, near[1], up)
    go(2, near[1], down)
    arrival(0, near[2])
    go(1, near[2], up)
    go(2, near[2], down)
    arrival(0, mirror)
    for off in (2, 1, 3):
        go(0, mirror, peer(off))
    go(1, mirror, up)
    go(2, mirror, down)
    for who in far:
        arrival(0, who)
        go(1, who, up)
        go(2, who, down)

    def chunk_in(i, carry):
        side = lax.rem(zh + i // 4, 2)
        who = side * 4 + lax.rem(xi + lax.rem(i, 4), 4)
        arrival(1, who)
        arrival(2, who)
        lhs = jnp.concatenate([tab[0, who], tab[1, who], tab[2, who]], 1)

        def keep(pos, value):
            rot[pl.ds(pl.multiple_of(pos * 128 + who * 16, 16), 16), :] = value.astype(BF16)

        rotate_in(dot(lhs, gat[...]), wige, feats, keep)
        return carry

    lax.fori_loop(0, 8, chunk_in, 0)
    for copy in sends:
        copy.wait_send()

    w0 = jnp.concatenate([w0_ref[:, lev].reshape(112, 128) for lev in range(7)], 1)
    y0 = dot(w0, rot[0:896, :])
    ys[0:7] = y0.reshape(7, 16, EDGES)
    for ref, n, start in ((w1_ref, 6, 7), (w2_ref, 5, 19)):
        lhs = jnp.concatenate(
            [ref[:, :, lev].reshape(2 * n * 16, 128) for lev in range(n)], 1
        )
        plus = rot[start * 128 : (start + n) * 128, :]
        minus = rot[(start + n) * 128 : (start + 2 * n) * 128, :]
        both = dot(lhs, jnp.concatenate([plus, minus], 1))
        half = n * 16
        ys[start : start + n] = (both[:half, :128] - both[half:, 128:]).reshape(n, 16, EDGES)
        ys[start + n : start + 2 * n] = (both[:half, 128:] + both[half:, :128]).reshape(
            n, 16, EDGES
        )

    attn = jnp.zeros((16, EDGES), F32)
    rows = iota((16, EDGES), 0)
    for t in range(16):
        attn = jnp.where(rows == t, attn_ref[t], attn)
    scalar = ys[0]
    gate = jax.nn.sigmoid(scalar)
    score = jnp.sum(scalar * gate * attn, axis=0, keepdims=True)
    live = jnp.broadcast_to((lane // 16) < count, (8, EDGES))
    score = jnp.broadcast_to(score, (8, EDGES))
    masked = jnp.where(live, score, -1e30)
    top = masked
    for shift in (16, 32, 64):
        top = jnp.maximum(top, spin(top, shift))
    weight = jnp.exp(jnp.where(live, score - top, -1e30))
    total = weight
    for shift in (16, 32, 64):
        total = total + spin(total, shift)
    weight = weight / total
    weight2 = jnp.concatenate([weight, weight], 0)
    inner = ys[0] * ps[0]
    for pos in range(1, 29):
        inner = inner + ys[pos] * ps[pos]
    dweight = jnp.broadcast_to(jnp.sum(inner * gate, axis=0, keepdims=True), (8, EDGES))
    mean = weight * dweight
    for shift in (16, 32, 64):
        mean = mean + spin(mean, shift)
    dscore = weight * (dweight - mean)
    dscore2 = jnp.concatenate([dscore, dscore], 0)
    slope = gate * (1.0 - gate)
    dscalar = weight2 * inner * slope + dscore2 * attn * (gate + scalar * slope)
    factor = weight2 * gate

    nil = jnp.zeros((16, EDGES), F32)
    dys = [ps[pos] * factor for pos in range(29)]
    dys[0] = dys[0] + dscalar
    dy0 = jnp.concatenate(dys[0:7] + [nil], 0).astype(BF16)
    drot[0:896, :] = dot(wt0[...], dy0).astype(BF16)
    for out, n, start in ((wt1, 6, 7), (wt2, 5, 19)):
        plus = jnp.concatenate(dys[start : start + n] + [nil] * (8 - n), 0).astype(BF16)
        minus = jnp.concatenate(dys[start + n : start + 2 * n] + [nil] * (8 - n), 0).astype(BF16)
        rhs = jnp.concatenate(
            [jnp.concatenate([plus, minus], 1), jnp.concatenate([minus, -plus], 1)], 0
        )
        both = dot(out[...], rhs)
        drot[start * 128 : (start + n) * 128, :] = both[:, :128].astype(BF16)
        drot[(start + n) * 128 : (start + 2 * n) * 128, :] = both[:, 128:].astype(BF16)

    def group_of(i):
        off = jnp.where(i < 2, 2, jnp.where(i < 4, 1, jnp.where(i < 6, 3, 0)))
        return lax.rem(i, 2) * 4 + lax.rem(xi + off, 4)

    def to_down(i):
        return rcopy(
            below_out.at[i], from_above.at[i], ghost_send.at[0, i], ghost_recv.at[0, i], down
        )

    def to_up(i):
        return rcopy(
            above_out.at[i], from_below.at[i], ghost_send.at[1, i], ghost_recv.at[1, i], up
        )

    def chunk_out(i, carry):
        who = group_of(i)

        def read(pos):
            value = drot[pl.ds(pl.multiple_of(pos * 128 + who * 16, 16), 16), :].astype(F32)
            return value[0:8], value[8:16]

        rotate_out(read, wige, back)
        out = dot(across(back).astype(BF16), sca[...])
        accum[i] = out[:, 0:128]
        below_out[i] = out[:, 128:256].astype(BF16)
        above_out[i] = out[:, 256:384].astype(BF16)
        to_down(i).start()
        to_up(i).start()
        return carry

    lax.fori_loop(0, 8, chunk_out, 0)

    def to_peer(i, off):
        return rcopy(x_out.at[i], x_in.at[i], xs_send.at[i], xs_recv.at[i], peer(off))

    def finish(i):
        to_down(i).wait_recv()
        to_up(i).wait_recv()
        return accum[i] + from_above[i].astype(F32) + from_below[i].astype(F32)

    for i in range(6):
        x_out[i] = finish(i).astype(BF16)
        to_peer(i, (2, 2, 1, 1, 3, 3)[i]).start()
    for i in (6, 7):
        red[i - 6] = finish(i)

    def read_z(pos):
        value = ys[pos] * factor
        return value[0:8], value[8:16]

    rotate_out(read_z, wige, back)
    wide = across(back)
    first = wide.astype(BF16)
    second = (wide - first.astype(F32)).astype(BF16)
    agg = dot(first, sca_tile[...]) + dot(second, sca_tile[...])
    upd_ref[...] = (x_ref[...].astype(F32) + from_rows(agg)).astype(BF16)

    for i in range(6):
        to_peer(i, (2, 2, 1, 1, 3, 3)[i]).wait_recv()
        red[i % 2] = red[i % 2] + x_in[i].astype(F32)
    z_out[...] = red[1 - zh].astype(BF16)
    across_z = rcopy(z_out, z_in, zs_send.at[0], zs_recv.at[0], other)
    across_z.start()
    across_z.wait_recv()
    grad = red[zh] + z_in[...].astype(F32)
    grad_ref[...] = g_ref[...].astype(F32) + from_rows(grad)

    across_z.wait_send()
    for i in range(6):
        to_peer(i, (2, 2, 1, 1, 3, 3)[i]).wait_send()
    for i in range(8):
        to_down(i).wait_send()
        to_up(i).wait_send()


def on_device(
    node_irreps,
    out_grad,
    edge_source,
    edge_rotation,
    edge_count,
    ghost_slot,
    wigner,
    so2_m0,
    so2_m1,
    so2_m2,
    attn_vector,
):
    vmem = pl.BlockSpec(memory_space=pltpu.VMEM)
    smem = pl.BlockSpec(memory_space=pltpu.SMEM)
    block = (ROWS, 128)
    dma = pltpu.SemaphoreType.DMA
    upd, grad = pl.pallas_call(
        body,
        out_shape=(
            jax.ShapeDtypeStruct((16, 16, K), BF16),
            jax.ShapeDtypeStruct((16, 16, K), F32),
        ),
        in_specs=[vmem, vmem, vmem, vmem, smem, smem, vmem, vmem, vmem, vmem, smem],
        out_specs=(vmem, vmem),
        scratch_shapes=[
            pltpu.VMEM((3, 8) + block, BF16),
            pltpu.VMEM((256, 128), F32),
            pltpu.VMEM((455, EDGES), F32),
            pltpu.VMEM((384, 1024), BF16),
            pltpu.VMEM((1024, 384), BF16),
            pltpu.VMEM((128, 1024), BF16),
            pltpu.VMEM((1024, 128), BF16),
            pltpu.VMEM((8 * PITCH, 128), F32),
            pltpu.VMEM((8 * PITCH, 128), F32),
            pltpu.VMEM((29 * 128, EDGES), BF16),
            pltpu.VMEM((29 * 128, EDGES), BF16),
            pltpu.VMEM((29, 16, EDGES), F32),
            pltpu.VMEM((29, 16, EDGES), F32),
            pltpu.VMEM((896, 128), BF16),
            pltpu.VMEM((768, 256), BF16),
            pltpu.VMEM((640, 256), BF16),
            pltpu.VMEM((8,) + block, F32),
            pltpu.VMEM((8,) + block, BF16),
            pltpu.VMEM((8,) + block, BF16),
            pltpu.VMEM((8,) + block, BF16),
            pltpu.VMEM((8,) + block, BF16),
            pltpu.VMEM((6,) + block, BF16),
            pltpu.VMEM((6,) + block, BF16),
            pltpu.VMEM(block, BF16),
            pltpu.VMEM(block, BF16),
            pltpu.VMEM((2,) + block, F32),
            dma((25,)),
            dma((3, 8)),
            dma((2, 8)),
            dma((2, 8)),
            dma((6,)),
            dma((6,)),
            dma((1,)),
            dma((1,)),
        ],
        compiler_params=pltpu.CompilerParams(
            collective_id=0, has_side_effects=True, vmem_limit_bytes=56 * 1024 * 1024
        ),
        name="layer",
    )(
        jnp.transpose(node_irreps, (1, 2, 0)),
        jnp.transpose(out_grad, (1, 2, 0)),
        edge_source,
        edge_rotation,
        edge_count,
        ghost_slot,
        wigner,
        jnp.transpose(so2_m0, (0, 2, 1, 3)),
        jnp.transpose(so2_m1, (0, 1, 3, 2, 4)),
        jnp.transpose(so2_m2, (0, 1, 3, 2, 4)),
        attn_vector,
    )
    return jnp.transpose(upd, (2, 0, 1)), jnp.transpose(grad, (2, 0, 1))


def solution(mesh):
    placed = (
        P(None, "ch", "dom"),
        P(None, "ch", "dom"),
        P(None, "dom"),
        P(None, "dom"),
        P("dom"),
        P("dom"),
        P(None, "dom"),
        P(None, "ch", None, None),
        P(None, None, "ch", None, None),
        P(None, None, "ch", None, None),
        P("ch"),
    )
    return jax.shard_map(
        on_device,
        mesh=mesh,
        in_specs=placed,
        out_specs=(P(None, "ch", "dom"), P(None, "ch", "dom")),
        check_vma=False,
    )
```

profile of v0, /device:TPU:4, one launch (start us, length us, event | category | flops | bytes accessed | tf_op | source)
XLA Modules:
  0.0 47.7 jit_solution(9542885965218136643)
XLA Ops:
  0.6 44.9 %layer.1 = (bf16[16,16,49]{2,1,0:T(8,128)(2,1)}, f32[16,16,49]{2,1,0:T(8,128)}) custom-call(bf16[16,16,49]{2,1,0:T(8,128)(2,1)} %bitcast.11, bf16[16,16,49]{2,1,0:T(8,128)(2,1)} %bitcast.12, s32[8,16]{1,0:T(8,128)} %src_ref.1, s32[8,16]{1,0:T(8,128)} %turn_ref.1, s32[16]{0:T(128)} %cnt_ref.1, s32[16]{0:T(128)} %slot_ref.1, f32[455,256]{1,0:T(8,128)} %wig_ref.1, ...), custom_call_target="tpu_custom_call" | custom-call | tf_op jit(solution)/shard_map/layer/pallas_call | solution.py:484
  45.6 0.0 copy-start
  45.6 1.5 %copy.15 = bf16[49,16,16]{0,2,1:T(8,128)(2,1)} copy(bf16[49,16,16]{0,2,1:T(8,128)(2,1)} %bitcast.13) | data formatting | bytes 50176
  47.1 0.0 copy-done
  47.1 0.7 %copy.16 = f32[49,16,16]{0,2,1:T(8,128)} copy(f32[49,16,16]{0,2,1:T(8,128)S(1)} %bitcast.10) | data formatting | bytes 100352
Async XLA Ops:
  45.6 1.5 %copy-start = (f32[16,16,49]{2,1,0:T(8,128)S(1)}, f32[16,16,49]{2,1,0:T(8,128)}, u32[]{:S(2)}) copy-start(f32[16,16,49]{2,1,0:T(8,128)} %get-tuple-element.5) | copy-start | bytes 150532
where the time goes:
time: 47.9 us; the launch traced here: 47.7 us
  Pallas kernels  44.9 us (94%)
  local copies, waits for them, and re-layouts  2.17 us (5%)
  between operations  0.65 us (1%)
    pallas_call x1, Pallas kernels, on_device(): pl.pallas_call(body, out_shape=(jax.ShapeDtypeStruct((16, 16, K), BF16),...  44.9 us
    unnamed x4, local copies, waits for them, and re-layouts  2.17 us

commit v1 on v0

--- a/solution.py
+++ b/solution.py
@@ -121,6 +121,19 @@
 
 
 def body(
+    x_hbm,
+    g_hbm,
+    src_hbm,
+    turn_hbm,
+    cnt_hbm,
+    slot_hbm,
+    wig_hbm,
+    w0_hbm,
+    w1_hbm,
+    w2_hbm,
+    attn_hbm,
+    upd_ref,
+    grad_ref,
     x_ref,
     g_ref,
     src_ref,
@@ -132,8 +145,7 @@
     w1_ref,
     w2_ref,
     attn_ref,
-    upd_ref,
-    grad_ref,
+    load_sem,
     tab,
     pad,
     wige,
@@ -185,6 +197,27 @@
     for target in (up, down, other, peer(1), peer(2), peer(3)):
         pl.semaphore_signal(barrier, inc=1, device_id=target, device_id_type=MESH)
 
+    loads = [
+        pltpu.make_async_copy(src, dst, load_sem.at[n])
+        for n, (src, dst) in enumerate(
+            (
+                (x_hbm, x_ref),
+                (src_hbm, src_ref),
+                (turn_hbm, turn_ref),
+                (cnt_hbm, cnt_ref),
+                (slot_hbm, slot_ref),
+                (wig_hbm, wig_ref),
+                (g_hbm, g_ref),
+                (w0_hbm, w0_ref),
+                (w1_hbm, w1_ref),
+                (w2_hbm, w2_ref),
+                (attn_hbm, attn_ref),
+            )
+        )
+    ]
+    for load in loads:
+        load.start()
+    loads[0].wait()
     tab[0, ch] = to_rows(x_ref, pad).astype(BF16)
 
     def rcopy(src, dst, ssem, rsem, target):
@@ -220,6 +253,9 @@
         go(0, ch, peer(off))
     go(1, ch, up)
     go(2, ch, down)
+
+    for load in loads[1:6]:
+        load.wait()
 
     spread = one_where(lax.rem(iota((16, EDGES), 1), 16) == iota((16, EDGES), 0))
     pick = (iota((8, EDGES), 1) // 16) == iota((8, EDGES), 0)
@@ -266,6 +302,9 @@
     second = rest.astype(BF16)
     third = (rest - second.astype(F32)).astype(BF16)
     wige[...] = dot(first, chosen) + (dot(second, chosen) + dot(third, chosen))
+
+    for load in loads[6:]:
+        load.wait()
 
     def keep_p(pos, value):
         ps[pos] = value
@@ -390,8 +429,10 @@
         drot[(start + n) * 128 : (start + 2 * n) * 128, :] = both[:, 128:].astype(BF16)
 
     def group_of(i):
-        off = jnp.where(i < 2, 2, jnp.where(i < 4, 1, jnp.where(i < 6, 3, 0)))
-        return lax.rem(i, 2) * 4 + lax.rem(xi + off, 4)
+        half = i // 4
+        j = lax.rem(i, 4)
+        off = jnp.where(j == 0, 2, jnp.where(j == 1, 1, jnp.where(j == 2, 3, 0)))
+        return lax.rem(1 - zh + half, 2) * 4 + lax.rem(xi + off, 4)
 
     def to_down(i):
         return rcopy(
@@ -429,11 +470,23 @@
         to_up(i).wait_recv()
         return accum[i] + from_above[i].astype(F32) + from_below[i].astype(F32)
 
-    for i in range(6):
-        x_out[i] = finish(i).astype(BF16)
-        to_peer(i, (2, 2, 1, 1, 3, 3)[i]).start()
-    for i in (6, 7):
-        red[i - 6] = finish(i)
+    offs = (2, 1, 3)
+    for half in range(2):
+        for j in range(3):
+            x_out[half * 3 + j] = finish(half * 4 + j).astype(BF16)
+            to_peer(half * 3 + j, offs[j]).start()
+        red[half] = finish(half * 4 + 3)
+
+    def gathered(half):
+        total = red[half]
+        for j in range(3):
+            to_peer(half * 3 + j, offs[j]).wait_recv()
+            total = total + x_in[half * 3 + j].astype(F32)
+        return total
+
+    z_out[...] = gathered(0).astype(BF16)
+    across_z = rcopy(z_out, z_in, zs_send.at[0], zs_recv.at[0], other)
+    across_z.start()
 
     def read_z(pos):
         value = ys[pos] * factor
@@ -444,21 +497,16 @@
     first = wide.astype(BF16)
     second = (wide - first.astype(F32)).astype(BF16)
     agg = dot(first, sca_tile[...]) + dot(second, sca_tile[...])
-    upd_ref[...] = (x_ref[...].astype(F32) + from_rows(agg)).astype(BF16)
-
-    for i in range(6):
-        to_peer(i, (2, 2, 1, 1, 3, 3)[i]).wait_recv()
-        red[i % 2] = red[i % 2] + x_in[i].astype(F32)
-    z_out[...] = red[1 - zh].astype(BF16)
-    across_z = rcopy(z_out, z_in, zs_send.at[0], zs_recv.at[0], other)
-    across_z.start()
+    upd_ref[...] = from_rows(agg)
+
+    kept = gathered(1)
     across_z.wait_recv()
-    grad = red[zh] + z_in[...].astype(F32)
-    grad_ref[...] = g_ref[...].astype(F32) + from_rows(grad)
+    grad = kept + z_in[...].astype(F32)
+    grad_ref[...] = from_rows(grad)
 
     across_z.wait_send()
     for i in range(6):
-        to_peer(i, (2, 2, 1, 1, 3, 3)[i]).wait_send()
+        to_peer(i, offs[i % 3]).wait_send()
     for i in range(8):
         to_down(i).wait_send()
         to_up(i).wait_send()
@@ -478,18 +526,30 @@
     attn_vector,
 ):
     vmem = pl.BlockSpec(memory_space=pltpu.VMEM)
-    smem = pl.BlockSpec(memory_space=pltpu.SMEM)
+    hbm = pl.BlockSpec(memory_space=pltpu.HBM)
     block = (ROWS, 128)
     dma = pltpu.SemaphoreType.DMA
     upd, grad = pl.pallas_call(
         body,
         out_shape=(
-            jax.ShapeDtypeStruct((16, 16, K), BF16),
+            jax.ShapeDtypeStruct((16, 16, K), F32),
             jax.ShapeDtypeStruct((16, 16, K), F32),
         ),
-        in_specs=[vmem, vmem, vmem, vmem, smem, smem, vmem, vmem, vmem, vmem, smem],
+        in_specs=[hbm] * 11,
         out_specs=(vmem, vmem),
         scratch_shapes=[
+            pltpu.VMEM((16, 16, K), BF16),
+            pltpu.VMEM((16, 16, K), BF16),
+            pltpu.VMEM((8, 16), jnp.int32),
+            pltpu.VMEM((8, 16), jnp.int32),
+            pltpu.SMEM((16,), jnp.int32),
+            pltpu.SMEM((16,), jnp.int32),
+            pltpu.VMEM((455, 256), F32),
+            pltpu.VMEM((7, 7, 16, 128), BF16),
+            pltpu.VMEM((2, 6, 6, 16, 128), BF16),
+            pltpu.VMEM((2, 5, 5, 16, 128), BF16),
+            pltpu.SMEM((16,), F32),
+            dma((11,)),
             pltpu.VMEM((3, 8) + block, BF16),
             pltpu.VMEM((256, 128), F32),
             pltpu.VMEM((455, EDGES), F32),
@@ -526,23 +586,30 @@
             dma((1,)),
         ],
         compiler_params=pltpu.CompilerParams(
-            collective_id=0, has_side_effects=True, vmem_limit_bytes=56 * 1024 * 1024
+            collective_id=0, has_side_effects=True, vmem_limit_bytes=24 * 1024 * 1024
         ),
         name="layer",
     )(
-        jnp.transpose(node_irreps, (1, 2, 0)),
-        jnp.transpose(out_grad, (1, 2, 0)),
-        edge_source,
-        edge_rotation,
-        edge_count,
-        ghost_slot,
-        wigner,
-        jnp.transpose(so2_m0, (0, 2, 1, 3)),
-        jnp.transpose(so2_m1, (0, 1, 3, 2, 4)),
-        jnp.transpose(so2_m2, (0, 1, 3, 2, 4)),
-        attn_vector,
+        *(
+            pltpu.with_memory_space_constraint(array, pltpu.HBM)
+            for array in (
+                jnp.transpose(node_irreps, (1, 2, 0)),
+                jnp.transpose(out_grad, (1, 2, 0)),
+                edge_source,
+                edge_rotation,
+                edge_count,
+                ghost_slot,
+                wigner,
+                jnp.transpose(so2_m0, (0, 2, 1, 3)),
+                jnp.transpose(so2_m1, (0, 1, 3, 2, 4)),
+                jnp.transpose(so2_m2, (0, 1, 3, 2, 4)),
+                attn_vector,
+            )
+        )
     )
-    return jnp.transpose(upd, (2, 0, 1)), jnp.transpose(grad, (2, 0, 1))
+    updated = node_irreps.astype(F32) + jnp.transpose(upd, (2, 0, 1))
+    irreps_grad = out_grad.astype(F32) + jnp.transpose(grad, (2, 0, 1))
+    return updated.astype(BF16), irreps_grad
 
 
 def solution(mesh):

time: 47.9 us -> 43.5 us (0.908)
  the two profiles are of different devices: /device:TPU:4 before, /device:TPU:2 now
where the time goes in v1:
time: 43.5 us; the launch traced here: 43.4 us
  Pallas kernels  42 us (97%)
  other arithmetic  0.7 us (2%)
  between operations  0.67 us (2%)
    pallas_call x1, Pallas kernels, on_device(): pl.pallas_call(body, out_shape=(jax.ShapeDtypeStruct((16, 16, K), F32), j...  42 us

profile of v1, /device:TPU:2, one launch (start us, length us, event | category | flops | bytes accessed | tf_op | source)
XLA Modules:
  0.0 43.4 jit_solution(10656056067413744913)
XLA Ops:
  0.6 0.0 copy-start
  0.6 0.0 copy-start.1
  0.7 42.0 %layer.1 = (f32[16,16,49]{2,1,0:T(8,128)S(1)}, f32[16,16,49]{2,1,0:T(8,128)S(1)}) custom-call(bf16[16,16,49]{2,1,0:T(8,128)(2,1)} %bitcast.12, bf16[16,16,49]{2,1,0:T(8,128)(2,1)} %bitcast.13, s32[8,16]{1,0:T(8,128)} %src_hbm.1, s32[8,16]{1,0:T(8,128)} %turn_hbm.1, s32[16]{0:T(128)} %cnt_hbm.1, s32[16]{0:T(128)} %slot_hbm.1, f32[455,256]{1,0:T(8,128)} %wig_hbm.1, ...), custom_call_target="tpu_custom_call" | custom-call | tf_op jit(solution)/shard_map/layer/pallas_call | solution.py:532
  42.7 0.0 copy-done
  42.7 0.0 copy-done.1
  42.7 0.7 %bitcast_add_fusion = (f32[49,16,16]{0,2,1:T(8,128)}, bf16[49,16,16]{0,2,1:T(8,128)(2,1)}) fusion(f32[16,16,49]{2,1,0:T(8,128)S(1)} %get-tuple-element.5, bf16[49,16,16]{0,2,1:T(8,128)(2,1)S(1)} %copy-done.1, f32[16,16,49]{2,1,0:T(8,128)S(1)} %get-tuple-element.4, bf16[49,16,16]{0,2,1:T(8,128)(2,1)S(1)} %copy-done), kind=kLoop, calls=%fused_computation | loop fusion | flops 62720 | bytes 225792 | tf_op jit(solution)/shard_map/add | solution.py:611
Async XLA Ops:
  0.6 42.0 %copy-start = (bf16[49,16,16]{0,2,1:T(8,128)(2,1)S(1)}, bf16[49,16,16]{0,2,1:T(8,128)(2,1)}, u32[]{:S(2)}) copy-start(bf16[49,16,16]{0,2,1:T(8,128)(2,1)} %param.11) | copy-start | bytes 75268
  0.6 42.0 %copy-start.1 = (bf16[49,16,16]{0,2,1:T(8,128)(2,1)S(1)}, bf16[49,16,16]{0,2,1:T(8,128)(2,1)}, u32[]{:S(2)}) copy-start(bf16[49,16,16]{0,2,1:T(8,128)(2,1)} %param.12) | copy-start | bytes 75268

commit v2 on v1

--- a/solution.py
+++ b/solution.py
@@ -67,42 +67,58 @@
 
 
 def rotate_in(mixed, wige, feats, write):
-    for c in range(8):
-        feats[c * PITCH : c * PITCH + ROWS, :] = mixed[:, c * EDGES : (c + 1) * EDGES]
+    groups = range(mixed.shape[0] // ROWS)
+    for n in groups:
+        for c in range(8):
+            feats[n, c * PITCH : c * PITCH + ROWS, :] = mixed[
+                n * ROWS : (n + 1) * ROWS, c * EDGES : (c + 1) * EDGES
+            ]
     for level, width, offset, orders in LEVELS:
         acc = {}
         for col in range(width):
             k = level * level + col
-            low = feats[pl.ds(k, 8, stride=PITCH), :]
-            high = feats[pl.ds(KP + k, 8, stride=PITCH), :]
+            parts = [
+                feats[n, pl.ds(start + k, 8, stride=PITCH), :] for n in groups for start in (0, KP)
+            ]
             for order in orders:
                 w = turn(wige, level, width, offset, order, col)
                 if col == 0:
-                    acc[order] = (w * low, w * high)
+                    acc[order] = [w * part for part in parts]
                 else:
-                    a, b = acc[order]
-                    acc[order] = (a + w * low, b + w * high)
+                    acc[order] = [old + w * part for old, part in zip(acc[order], parts)]
         for order in orders:
-            write(place(level, order), jnp.concatenate(acc[order], 0))
-
-
-def rotate_out(read, wige, back):
+            for n in groups:
+                write(n, place(level, order), jnp.concatenate(acc[order][2 * n : 2 * n + 2], 0))
+
+
+def rotate_out(read, wige, back, count):
     for level, width, offset, orders in LEVELS:
-        mine = {order: read(place(level, order)) for order in orders}
+        mine = {
+            order: [part for n in range(count) for part in read(n, place(level, order))]
+            for order in orders
+        }
         for col in range(width):
             k = level * level + col
-            low = high = None
+            total = None
             for order in orders:
                 w = turn(wige, level, width, offset, order, col)
-                a, b = mine[order]
-                low = w * a if low is None else low + w * a
-                high = w * b if high is None else high + w * b
-            back[pl.ds(k, 8, stride=PITCH), :] = low
-            back[pl.ds(KP + k, 8, stride=PITCH), :] = high
-
-
-def across(back):
-    return jnp.concatenate([back[c * PITCH : c * PITCH + ROWS, :] for c in range(8)], 1)
+                if total is None:
+                    total = [w * part for part in mine[order]]
+                else:
+                    total = [old + w * part for old, part in zip(total, mine[order])]
+            for n in range(count):
+                back[n, pl.ds(k, 8, stride=PITCH), :] = total[2 * n]
+                back[n, pl.ds(KP + k, 8, stride=PITCH), :] = total[2 * n + 1]
+
+
+def across(back, count):
+    return jnp.concatenate(
+        [
+            jnp.concatenate([back[n, c * PITCH : c * PITCH + ROWS, :] for c in range(8)], 1)
+            for n in range(count)
+        ],
+        0,
+    )
 
 
 def to_rows(ref, pad):
@@ -163,8 +179,7 @@
     wt1,
     wt2,
     accum,
-    below_out,
-    above_out,
+    ghost_out,
     from_above,
     from_below,
     x_out,
@@ -172,6 +187,9 @@
     z_out,
     z_in,
     red,
+    end_x,
+    end_sum,
+    end_got,
     send_sem,
     tab_sem,
     ghost_send,
@@ -180,22 +198,46 @@
     xs_recv,
     zs_send,
     zs_recv,
+    end_send,
+    end_recv,
+    end_last,
 ):
     doms = lax.axis_size("dom")
     d = lax.axis_index("dom")
     ch = lax.axis_index("ch")
     zh = ch // 4
     xi = lax.rem(ch, 4)
+    mirror = lax.rem(ch + 4, 8)
     up = (lax.rem(d + 1, doms), ch)
     down = (lax.rem(d + doms - 1, doms), ch)
-    other = (d, lax.rem(ch + 4, 8))
+    other = (d, mirror)
 
     def peer(off):
         return (d, zh * 4 + lax.rem(xi + off, 4))
 
+    has_up = d != doms - 1
+    has_down = d != 0
+    end = jnp.logical_or(d == 0, d == doms - 1)
+    first_end = (doms - 1 - d, ch)
+    second_end = (doms - 1 - d, mirror)
+    end_in = jnp.where(d == 0, 1, 2)
+    end_out = jnp.where(d == 0, 2, 1)
+    end_side = jnp.where(d == 0, 0, 1)
+
     barrier = pltpu.get_barrier_semaphore()
-    for target in (up, down, other, peer(1), peer(2), peer(3)):
+
+    def greet(target):
         pl.semaphore_signal(barrier, inc=1, device_id=target, device_id_type=MESH)
+
+    for target in (other, peer(1), peer(2), peer(3)):
+        greet(target)
+    pl.when(has_up)(lambda: greet(up))
+    pl.when(has_down)(lambda: greet(down))
+
+    @pl.when(end)
+    def _():
+        greet(first_end)
+        greet(second_end)
 
     loads = [
         pltpu.make_async_copy(src, dst, load_sem.at[n])
@@ -240,19 +282,27 @@
             tab.at[0, who], tab.at[blk, who], send_sem.at[0], tab_sem.at[blk, who], up
         ).wait_recv()
 
-    pl.semaphore_wait(barrier, 6)
+    pl.semaphore_wait(barrier, jnp.where(end, 7, 6))
     sends = []
 
-    def go(blk, who, target):
+    def go(blk, who, target, cond=None):
         copy = table_copy(blk, who, len(sends), target)
-        copy.start()
-        sends.append(copy)
+        if cond is None:
+            copy.start()
+        else:
+            pl.when(cond)(lambda: copy.start())
+        sends.append((copy, cond))
+
+    def halo(who):
+        go(1, who, up, has_up)
+        go(2, who, down, has_down)
 
     go(0, ch, other)
+    go(end_out, ch, second_end, end)
+    go(end_out, ch, first_end, end)
     for off in (2, 1, 3):
         go(0, ch, peer(off))
-    go(1, ch, up)
-    go(2, ch, down)
+    halo(ch)
 
     for load in loads[1:6]:
         load.wait()
@@ -306,7 +356,7 @@
     for load in loads[6:]:
         load.wait()
 
-    def keep_p(pos, value):
+    def keep_p(n, pos, value):
         ps[pos] = value
 
     rotate_in(dot(to_rows(g_ref, pad).astype(BF16), gat_tile[...]), wige, feats, keep_p)
@@ -328,42 +378,69 @@
 
     near = [zh * 4 + lax.rem(xi + off, 4) for off in (1, 3, 2)]
     far = [(1 - zh) * 4 + lax.rem(xi + off, 4) for off in (1, 3, 2)]
-    mirror = lax.rem(ch + 4, 8)
     arrival(0, near[0])
-    go(1, near[0], up)
-    go(2, near[0], down)
+    halo(near[0])
     arrival(0, near[1])
-    go(1, near[1], up)
-    go(2, near[1], down)
+    halo(near[1])
     arrival(0, near[2])
-    go(1, near[2], up)
-    go(2, near[2], down)
+    halo(near[2])
+
+    def end_copy(n, who, target):
+        return rcopy(
+            tab.at[end_in, who],
+            tab.at[end_in, who],
+            end_send.at[n],
+            tab_sem.at[end_in, who],
+            target,
+        )
+
+    @pl.when(end)
+    def _():
+        for n, who in enumerate((mirror, ch)):
+            end_copy(0, who, first_end).wait_recv()
+            for j, off in enumerate((2, 1, 3)):
+                end_copy(n * 3 + j, who, peer(off)).start()
+
     arrival(0, mirror)
     for off in (2, 1, 3):
         go(0, mirror, peer(off))
-    go(1, mirror, up)
-    go(2, mirror, down)
+    halo(mirror)
     for who in far:
         arrival(0, who)
-        go(1, who, up)
-        go(2, who, down)
-
-    def chunk_in(i, carry):
-        side = lax.rem(zh + i // 4, 2)
-        who = side * 4 + lax.rem(xi + lax.rem(i, 4), 4)
-        arrival(1, who)
-        arrival(2, who)
-        lhs = jnp.concatenate([tab[0, who], tab[1, who], tab[2, who]], 1)
-
-        def keep(pos, value):
-            rot[pl.ds(pl.multiple_of(pos * 128 + who * 16, 16), 16), :] = value.astype(BF16)
+        halo(who)
+
+    def halo_arrival(blk, who):
+        came = jnp.logical_and(end, jnp.logical_and(lax.rem(who, 4) == xi, blk == end_in))
+        pl.when(jnp.logical_not(came))(lambda: arrival(blk, who))
+
+    def pair_in(i, carry):
+        side = lax.rem(zh + i // 2, 2)
+        both = [side * 4 + lax.rem(xi + lax.rem(2 * i, 4) + n, 4) for n in range(2)]
+        for who in both:
+            halo_arrival(1, who)
+            halo_arrival(2, who)
+        lhs = jnp.concatenate(
+            [jnp.concatenate([tab[0, who], tab[1, who], tab[2, who]], 1) for who in both], 0
+        )
+
+        def keep(n, pos, value):
+            rot[pl.ds(pl.multiple_of(pos * 128 + both[n] * 16, 16), 16), :] = value.astype(BF16)
 
         rotate_in(dot(lhs, gat[...]), wige, feats, keep)
         return carry
 
-    lax.fori_loop(0, 8, chunk_in, 0)
-    for copy in sends:
-        copy.wait_send()
+    lax.fori_loop(0, 4, pair_in, 0)
+    for copy, cond in sends:
+        if cond is None:
+            copy.wait_send()
+        else:
+            pl.when(cond)(lambda copy=copy: copy.wait_send())
+
+    @pl.when(end)
+    def _():
+        for n, who in enumerate((mirror, ch)):
+            for j, off in enumerate((2, 1, 3)):
+                end_copy(n * 3 + j, who, peer(off)).wait_send()
 
     w0 = jnp.concatenate([w0_ref[:, lev].reshape(112, 128) for lev in range(7)], 1)
     y0 = dot(w0, rot[0:896, :])
@@ -434,43 +511,83 @@
         off = jnp.where(j == 0, 2, jnp.where(j == 1, 1, jnp.where(j == 2, 3, 0)))
         return lax.rem(1 - zh + half, 2) * 4 + lax.rem(xi + off, 4)
 
-    def to_down(i):
+    def to_down(who):
         return rcopy(
-            below_out.at[i], from_above.at[i], ghost_send.at[0, i], ghost_recv.at[0, i], down
-        )
-
-    def to_up(i):
+            ghost_out.at[0, who],
+            from_above.at[who],
+            ghost_send.at[0, who],
+            ghost_recv.at[0, who],
+            down,
+        )
+
+    def to_up(who):
         return rcopy(
-            above_out.at[i], from_below.at[i], ghost_send.at[1, i], ghost_recv.at[1, i], up
-        )
-
-    def chunk_out(i, carry):
-        who = group_of(i)
-
-        def read(pos):
-            value = drot[pl.ds(pl.multiple_of(pos * 128 + who * 16, 16), 16), :].astype(F32)
+            ghost_out.at[1, who],
+            from_below.at[who],
+            ghost_send.at[1, who],
+            ghost_recv.at[1, who],
+            up,
+        )
+
+    def pair_out(i, carry):
+        both = [group_of(2 * i + n) for n in range(2)]
+
+        def read(n, pos):
+            start = pl.multiple_of(pos * 128 + both[n] * 16, 16)
+            value = drot[pl.ds(start, 16), :].astype(F32)
             return value[0:8], value[8:16]
 
-        rotate_out(read, wige, back)
-        out = dot(across(back).astype(BF16), sca[...])
-        accum[i] = out[:, 0:128]
-        below_out[i] = out[:, 128:256].astype(BF16)
-        above_out[i] = out[:, 256:384].astype(BF16)
-        to_down(i).start()
-        to_up(i).start()
+        rotate_out(read, wige, back, 2)
+        out = dot(across(back, 2).astype(BF16), sca[...])
+        for n, who in enumerate(both):
+            part = out[n * ROWS : (n + 1) * ROWS]
+            ghost_out[0, who] = part[:, 128:256].astype(BF16)
+            ghost_out[1, who] = part[:, 256:384].astype(BF16)
+            pl.when(has_down)(lambda who=who: to_down(who).start())
+            pl.when(has_up)(lambda who=who: to_up(who).start())
+            accum[who] = part[:, 0:128]
         return carry
 
-    lax.fori_loop(0, 8, chunk_out, 0)
+    @pl.when(d == doms - 1)
+    def _():
+        from_above[...] = jnp.zeros_like(from_above)
+
+    @pl.when(d == 0)
+    def _():
+        from_below[...] = jnp.zeros_like(from_below)
+
+    lax.fori_loop(0, 4, pair_out, 0)
+
+    offs = (2, 1, 3)
+
+    def end_peer(i):
+        half = i // 3
+        off = offs[i % 3]
+        who = ((zh + 1 - half) % 2) * 4 + lax.rem(xi + off, 4)
+        return rcopy(
+            ghost_out.at[end_side, who], end_x.at[i], end_send.at[i], end_recv.at[i], peer(off)
+        )
+
+    def end_home(half):
+        target = (second_end, first_end)[half]
+        return rcopy(
+            end_sum.at[half], end_got.at[half], end_last.at[half], end_last.at[2 + half], target
+        )
+
+    @pl.when(end)
+    def _():
+        for i in range(6):
+            end_peer(i).start()
 
     def to_peer(i, off):
         return rcopy(x_out.at[i], x_in.at[i], xs_send.at[i], xs_recv.at[i], peer(off))
 
     def finish(i):
-        to_down(i).wait_recv()
-        to_up(i).wait_recv()
-        return accum[i] + from_above[i].astype(F32) + from_below[i].astype(F32)
-
-    offs = (2, 1, 3)
+        who = group_of(i)
+        pl.when(has_up)(lambda: to_down(who).wait_recv())
+        pl.when(has_down)(lambda: to_up(who).wait_recv())
+        return accum[who] + from_above[who].astype(F32) + from_below[who].astype(F32)
+
     for half in range(2):
         for j in range(3):
             x_out[half * 3 + j] = finish(half * 4 + j).astype(BF16)
@@ -484,32 +601,57 @@
             total = total + x_in[half * 3 + j].astype(F32)
         return total
 
+    @pl.when(end)
+    def _():
+        for half in range(2):
+            who = ((zh + 1 - half) % 2) * 4 + xi
+            total = ghost_out[end_side, who].astype(F32)
+            for j in range(3):
+                end_peer(half * 3 + j).wait_recv()
+                total = total + end_x[half * 3 + j].astype(F32)
+            end_sum[half] = total.astype(BF16)
+            end_home(half).start()
+
     z_out[...] = gathered(0).astype(BF16)
     across_z = rcopy(z_out, z_in, zs_send.at[0], zs_recv.at[0], other)
     across_z.start()
 
-    def read_z(pos):
+    def read_z(n, pos):
         value = ys[pos] * factor
         return value[0:8], value[8:16]
 
-    rotate_out(read_z, wige, back)
-    wide = across(back)
+    rotate_out(read_z, wige, back, 1)
+    wide = across(back, 1)
     first = wide.astype(BF16)
     second = (wide - first.astype(F32)).astype(BF16)
     agg = dot(first, sca_tile[...]) + dot(second, sca_tile[...])
     upd_ref[...] = from_rows(agg)
 
-    kept = gathered(1)
+    red[1] = gathered(1)
+
+    @pl.when(end)
+    def _():
+        end_home(0).wait_recv()
+        end_home(1).wait_recv()
+        red[1] = red[1] + (end_got[0].astype(F32) + end_got[1].astype(F32))
+
     across_z.wait_recv()
-    grad = kept + z_in[...].astype(F32)
+    grad = red[1] + z_in[...].astype(F32)
     grad_ref[...] = from_rows(grad)
 
     across_z.wait_send()
     for i in range(6):
         to_peer(i, offs[i % 3]).wait_send()
     for i in range(8):
-        to_down(i).wait_send()
-        to_up(i).wait_send()
+        pl.when(has_down)(lambda i=i: to_down(i).wait_send())
+        pl.when(has_up)(lambda i=i: to_up(i).wait_send())
+
+    @pl.when(end)
+    def _():
+        for i in range(6):
+            end_peer(i).wait_send()
+        end_home(0).wait_send()
+        end_home(1).wait_send()
 
 
 def on_device(
@@ -557,8 +699,8 @@
             pltpu.VMEM((1024, 384), BF16),
             pltpu.VMEM((128, 1024), BF16),
             pltpu.VMEM((1024, 128), BF16),
-            pltpu.VMEM((8 * PITCH, 128), F32),
-            pltpu.VMEM((8 * PITCH, 128), F32),
+            pltpu.VMEM((2, 8 * PITCH, 128), F32),
+            pltpu.VMEM((2, 8 * PITCH, 128), F32),
             pltpu.VMEM((29 * 128, EDGES), BF16),
             pltpu.VMEM((29 * 128, EDGES), BF16),
             pltpu.VMEM((29, 16, EDGES), F32),
@@ -567,8 +709,7 @@
             pltpu.VMEM((768, 256), BF16),
             pltpu.VMEM((640, 256), BF16),
             pltpu.VMEM((8,) + block, F32),
-            pltpu.VMEM((8,) + block, BF16),
-            pltpu.VMEM((8,) + block, BF16),
+            pltpu.VMEM((2, 8) + block, BF16),
             pltpu.VMEM((8,) + block, BF16),
             pltpu.VMEM((8,) + block, BF16),
             pltpu.VMEM((6,) + block, BF16),
@@ -576,7 +717,10 @@
             pltpu.VMEM(block, BF16),
             pltpu.VMEM(block, BF16),
             pltpu.VMEM((2,) + block, F32),
-            dma((25,)),
+            pltpu.VMEM((6,) + block, BF16),
+            pltpu.VMEM((2,) + block, BF16),
+            pltpu.VMEM((2,) + block, BF16),
+            dma((27,)),
             dma((3, 8)),
             dma((2, 8)),
             dma((2, 8)),
@@ -584,6 +728,9 @@
             dma((6,)),
             dma((1,)),
             dma((1,)),
+            dma((6,)),
+            dma((6,)),
+            dma((4,)),
         ],
         compiler_params=pltpu.CompilerParams(
             collective_id=0, has_side_effects=True, vmem_limit_bytes=24 * 1024 * 1024

time: 43.5 us -> 41.3 us (0.949)
  Pallas kernels: 42 us -> 39.8 us
    pallas_call x1, Pallas kernels: 42 us -> 39.8 us  [on_device(): pl.pallas_call(body, out_shape=(jax.ShapeDtypeStruct((16, 16, K), F32), j...]
where the time goes in v2:
time: 41.3 us; the launch traced here: 41.1 us
  Pallas kernels  39.8 us (96%)
  other arithmetic  0.7 us (2%)
  between operations  0.67 us (2%)
    pallas_call x1, Pallas kernels, on_device(): pl.pallas_call(body, out_shape=(jax.ShapeDtypeStruct((16, 16, K), F32), j...  39.8 us

profile of v2, /device:TPU:2, one launch (start us, length us, event | category | flops | bytes accessed | tf_op | source)
XLA Modules:
  0.0 41.1 jit_solution(9663825555569128917)
XLA Ops:
  0.6 0.0 copy-start
  0.6 0.0 copy-start.1
  0.7 39.8 %layer.1 = (f32[16,16,49]{2,1,0:T(8,128)S(1)}, f32[16,16,49]{2,1,0:T(8,128)S(1)}) custom-call(bf16[16,16,49]{2,1,0:T(8,128)(2,1)} %bitcast.12, bf16[16,16,49]{2,1,0:T(8,128)(2,1)} %bitcast.13, s32[8,16]{1,0:T(8,128)} %src_hbm.1, s32[8,16]{1,0:T(8,128)} %turn_hbm.1, s32[16]{0:T(128)} %cnt_hbm.1, s32[16]{0:T(128)} %slot_hbm.1, f32[455,256]{1,0:T(8,128)} %wig_hbm.1, ...), custom_call_target="tpu_custom_call" | custom-call | tf_op jit(solution)/shard_map/layer/pallas_call | solution.py:674
  40.4 0.0 copy-done
  40.4 0.0 copy-done.1
  40.4 0.7 %bitcast_add_fusion = (f32[49,16,16]{0,2,1:T(8,128)}, bf16[49,16,16]{0,2,1:T(8,128)(2,1)}) fusion(f32[16,16,49]{2,1,0:T(8,128)S(1)} %get-tuple-element.5, bf16[49,16,16]{0,2,1:T(8,128)(2,1)S(1)} %copy-done.1, f32[16,16,49]{2,1,0:T(8,128)S(1)} %get-tuple-element.4, bf16[49,16,16]{0,2,1:T(8,128)(2,1)S(1)} %copy-done), kind=kLoop, calls=%fused_computation | loop fusion | flops 62720 | bytes 225792 | tf_op jit(solution)/shard_map/add | solution.py:758
Async XLA Ops:
  0.6 39.8 %copy-start = (bf16[49,16,16]{0,2,1:T(8,128)(2,1)S(1)}, bf16[49,16,16]{0,2,1:T(8,128)(2,1)}, u32[]{:S(2)}) copy-start(bf16[49,16,16]{0,2,1:T(8,128)(2,1)} %param.11) | copy-start | bytes 75268
  0.6 39.8 %copy-start.1 = (bf16[49,16,16]{0,2,1:T(8,128)(2,1)S(1)}, bf16[49,16,16]{0,2,1:T(8,128)(2,1)}, u32[]{:S(2)}) copy-start(bf16[49,16,16]{0,2,1:T(8,128)(2,1)} %param.12) | copy-start | bytes 75268

commit v3 on v2

--- a/solution.py
+++ b/solution.py
@@ -55,6 +55,13 @@
 
 def spin(x, shift):
     return pltpu.roll(x, shift, 1)
+
+
+def over_slots(x, join):
+    parts = [x] + [spin(x, shift) for shift in range(OWN, EDGES, OWN)]
+    while len(parts) > 1:
+        parts = [join(parts[i], parts[i + 1]) for i in range(0, len(parts), 2)]
+    return parts[0]
 
 
 def dot(a, b):
@@ -468,22 +475,15 @@
     live = jnp.broadcast_to((lane // 16) < count, (8, EDGES))
     score = jnp.broadcast_to(score, (8, EDGES))
     masked = jnp.where(live, score, -1e30)
-    top = masked
-    for shift in (16, 32, 64):
-        top = jnp.maximum(top, spin(top, shift))
+    top = over_slots(masked, jnp.maximum)
     weight = jnp.exp(jnp.where(live, score - top, -1e30))
-    total = weight
-    for shift in (16, 32, 64):
-        total = total + spin(total, shift)
-    weight = weight / total
+    weight = weight / over_slots(weight, jnp.add)
     weight2 = jnp.concatenate([weight, weight], 0)
     inner = ys[0] * ps[0]
     for pos in range(1, 29):
         inner = inner + ys[pos] * ps[pos]
     dweight = jnp.broadcast_to(jnp.sum(inner * gate, axis=0, keepdims=True), (8, EDGES))
-    mean = weight * dweight
-    for shift in (16, 32, 64):
-        mean = mean + spin(mean, shift)
+    mean = over_slots(weight * dweight, jnp.add)
     dscore = weight * (dweight - mean)
     dscore2 = jnp.concatenate([dscore, dscore], 0)
     slope = gate * (1.0 - gate)
@@ -635,11 +635,6 @@
         end_home(1).wait_recv()
         red[1] = red[1] + (end_got[0].astype(F32) + end_got[1].astype(F32))
 
-    across_z.wait_recv()
-    grad = red[1] + z_in[...].astype(F32)
-    grad_ref[...] = from_rows(grad)
-
-    across_z.wait_send()
     for i in range(6):
         to_peer(i, offs[i % 3]).wait_send()
     for i in range(8):
@@ -652,6 +647,10 @@
             end_peer(i).wait_send()
         end_home(0).wait_send()
         end_home(1).wait_send()
+    across_z.wait_send()
+    across_z.wait_recv()
+    grad = red[1] + z_in[...].astype(F32)
+    grad_ref[...] = from_rows(grad)
 
 
 def on_device(

time: 41.3 us -> 40.9 us (level)
  no operation moved by 1% of the time
where the time goes in v3:
time: 40.9 us; the launch traced here: 40.8 us
  Pallas kernels  39.4 us (96%)
  other arithmetic  0.7 us (2%)
  between operations  0.67 us (2%)
    pallas_call x1, Pallas kernels, on_device(): pl.pallas_call(body, out_shape=(jax.ShapeDtypeStruct((16, 16, K), F32), j...  39.4 us

profile of v3, /device:TPU:2, one launch (start us, length us, event | category | flops | bytes accessed | tf_op | source)
XLA Modules:
  0.0 40.8 jit_solution(5637866853989052106)
XLA Ops:
  0.6 0.0 copy-start
  0.6 0.0 copy-start.1
  0.7 39.4 %layer.1 = (f32[16,16,49]{2,1,0:T(8,128)S(1)}, f32[16,16,49]{2,1,0:T(8,128)S(1)}) custom-call(bf16[16,16,49]{2,1,0:T(8,128)(2,1)} %bitcast.12, bf16[16,16,49]{2,1,0:T(8,128)(2,1)} %bitcast.13, s32[8,16]{1,0:T(8,128)} %src_hbm.1, s32[8,16]{1,0:T(8,128)} %turn_hbm.1, s32[16]{0:T(128)} %cnt_hbm.1, s32[16]{0:T(128)} %slot_hbm.1, f32[455,256]{1,0:T(8,128)} %wig_hbm.1, ...), custom_call_target="tpu_custom_call" | custom-call | tf_op jit(solution)/shard_map/layer/pallas_call | solution.py:673
  40.0 0.0 copy-done
  40.0 0.0 copy-done.1
  40.1 0.7 %bitcast_add_fusion = (f32[49,16,16]{0,2,1:T(8,128)}, bf16[49,16,16]{0,2,1:T(8,128)(2,1)}) fusion(f32[16,16,49]{2,1,0:T(8,128)S(1)} %get-tuple-element.5, bf16[49,16,16]{0,2,1:T(8,128)(2,1)S(1)} %copy-done.1, f32[16,16,49]{2,1,0:T(8,128)S(1)} %get-tuple-element.4, bf16[49,16,16]{0,2,1:T(8,128)(2,1)S(1)} %copy-done), kind=kLoop, calls=%fused_computation | loop fusion | flops 62720 | bytes 225792 | tf_op jit(solution)/shard_map/add | solution.py:757
Async XLA Ops:
  0.6 39.4 %copy-start = (bf16[49,16,16]{0,2,1:T(8,128)(2,1)S(1)}, bf16[49,16,16]{0,2,1:T(8,128)(2,1)}, u32[]{:S(2)}) copy-start(bf16[49,16,16]{0,2,1:T(8,128)(2,1)} %param.11) | copy-start | bytes 75268
  0.6 39.4 %copy-start.1 = (bf16[49,16,16]{0,2,1:T(8,128)(2,1)S(1)}, bf16[49,16,16]{0,2,1:T(8,128)(2,1)}, u32[]{:S(2)}) copy-start(bf16[49,16,16]{0,2,1:T(8,128)(2,1)} %param.12) | copy-start | bytes 75268

commit v4 on v3

--- a/solution.py
+++ b/solution.py
@@ -491,19 +491,21 @@
     factor = weight2 * gate
 
     nil = jnp.zeros((16, EDGES), F32)
-    dys = [ps[pos] * factor for pos in range(29)]
-    dys[0] = dys[0] + dscalar
-    dy0 = jnp.concatenate(dys[0:7] + [nil], 0).astype(BF16)
-    drot[0:896, :] = dot(wt0[...], dy0).astype(BF16)
+    gated = [ps[pos] * gate for pos in range(29)]
     for out, n, start in ((wt1, 6, 7), (wt2, 5, 19)):
-        plus = jnp.concatenate(dys[start : start + n] + [nil] * (8 - n), 0).astype(BF16)
-        minus = jnp.concatenate(dys[start + n : start + 2 * n] + [nil] * (8 - n), 0).astype(BF16)
+        plus = jnp.concatenate(gated[start : start + n] + [nil] * (8 - n), 0).astype(BF16)
+        minus = jnp.concatenate(gated[start + n : start + 2 * n] + [nil] * (8 - n), 0).astype(BF16)
         rhs = jnp.concatenate(
             [jnp.concatenate([plus, minus], 1), jnp.concatenate([minus, -plus], 1)], 0
         )
         both = dot(out[...], rhs)
-        drot[start * 128 : (start + n) * 128, :] = both[:, :128].astype(BF16)
-        drot[(start + n) * 128 : (start + 2 * n) * 128, :] = both[:, 128:].astype(BF16)
+        tall = jnp.broadcast_to(weight[0:1], (n * 128, EDGES))
+        drot[start * 128 : (start + n) * 128, :] = (both[:, :128] * tall).astype(BF16)
+        drot[(start + n) * 128 : (start + 2 * n) * 128, :] = (both[:, 128:] * tall).astype(BF16)
+    dys = [gated[pos] * weight2 for pos in range(7)]
+    dys[0] = dys[0] + dscalar
+    dy0 = jnp.concatenate(dys + [nil], 0).astype(BF16)
+    drot[0:896, :] = dot(wt0[...], dy0).astype(BF16)
 
     def group_of(i):
         half = i // 4
@@ -528,6 +530,19 @@
             ghost_recv.at[1, who],
             up,
         )
+
+    offs = (2, 1, 3)
+
+    def end_part(i, who, target):
+        return rcopy(
+            ghost_out.at[end_side, who], end_x.at[i], end_send.at[i], end_recv.at[i], target
+        )
+
+    def end_peer(i):
+        half = i // 3
+        off = offs[i % 3]
+        who = ((zh + 1 - half) % 2) * 4 + lax.rem(xi + off, 4)
+        return end_part(i, who, peer(off))
 
     def pair_out(i, carry):
         both = [group_of(2 * i + n) for n in range(2)]
@@ -546,6 +561,17 @@
             pl.when(has_down)(lambda who=who: to_down(who).start())
             pl.when(has_up)(lambda who=who: to_up(who).start())
             accum[who] = part[:, 0:128]
+
+        odd = lax.rem(i, 2)
+
+        @pl.when(end)
+        def _():
+            end_part((i // 2) * 3 + odd * 2, both[0], peer(2 + odd)).start()
+
+        @pl.when(jnp.logical_and(end, odd == 0))
+        def _():
+            end_part((i // 2) * 3 + 1, both[1], peer(1)).start()
+
         return carry
 
     @pl.when(d == doms - 1)
@@ -557,16 +583,6 @@
         from_below[...] = jnp.zeros_like(from_below)
 
     lax.fori_loop(0, 4, pair_out, 0)
-
-    offs = (2, 1, 3)
-
-    def end_peer(i):
-        half = i // 3
-        off = offs[i % 3]
-        who = ((zh + 1 - half) % 2) * 4 + lax.rem(xi + off, 4)
-        return rcopy(
-            ghost_out.at[end_side, who], end_x.at[i], end_send.at[i], end_recv.at[i], peer(off)
-        )
 
     def end_home(half):
         target = (second_end, first_end)[half]
@@ -574,10 +590,6 @@
             end_sum.at[half], end_got.at[half], end_last.at[half], end_last.at[2 + half], target
         )
 
-    @pl.when(end)
-    def _():
-        for i in range(6):
-            end_peer(i).start()
 
     def to_peer(i, off):
         return rcopy(x_out.at[i], x_in.at[i], xs_send.at[i], xs_recv.at[i], peer(off))

time: 40.9 us -> 40.2 us (0.983)
  Pallas kernels: 39.4 us -> 38.6 us
    pallas_call x1, Pallas kernels: 39.4 us -> 38.6 us  [on_device(): pl.pallas_call(body, out_shape=(jax.ShapeDtypeStruct((16, 16, K), F32), j...]
where the time goes in v4:
time: 40.2 us; the launch traced here: 40 us
  Pallas kernels  38.6 us (96%)
  other arithmetic  0.7 us (2%)
  between operations  0.67 us (2%)
    pallas_call x1, Pallas kernels, on_device(): pl.pallas_call(body, out_shape=(jax.ShapeDtypeStruct((16, 16, K), F32), j...  38.6 us

profile of v4, /device:TPU:2, one launch (start us, length us, event | category | flops | bytes accessed | tf_op | source)
XLA Modules:
  0.0 40.0 jit_solution(12456382216869822952)
XLA Ops:
  0.6 0.0 copy-start
  0.6 0.0 copy-start.1
  0.7 38.6 %layer.1 = (f32[16,16,49]{2,1,0:T(8,128)S(1)}, f32[16,16,49]{2,1,0:T(8,128)S(1)}) custom-call(bf16[16,16,49]{2,1,0:T(8,128)(2,1)} %bitcast.12, bf16[16,16,49]{2,1,0:T(8,128)(2,1)} %bitcast.13, s32[8,16]{1,0:T(8,128)} %src_hbm.1, s32[8,16]{1,0:T(8,128)} %turn_hbm.1, s32[16]{0:T(128)} %cnt_hbm.1, s32[16]{0:T(128)} %slot_hbm.1, f32[455,256]{1,0:T(8,128)} %wig_hbm.1, ...), custom_call_target="tpu_custom_call" | custom-call | tf_op jit(solution)/shard_map/layer/pallas_call | solution.py:685
  39.3 0.0 copy-done
  39.3 0.0 copy-done.1
  39.3 0.7 %bitcast_add_fusion = (f32[49,16,16]{0,2,1:T(8,128)}, bf16[49,16,16]{0,2,1:T(8,128)(2,1)}) fusion(f32[16,16,49]{2,1,0:T(8,128)S(1)} %get-tuple-element.5, bf16[49,16,16]{0,2,1:T(8,128)(2,1)S(1)} %copy-done.1, f32[16,16,49]{2,1,0:T(8,128)S(1)} %get-tuple-element.4, bf16[49,16,16]{0,2,1:T(8,128)(2,1)S(1)} %copy-done), kind=kLoop, calls=%fused_computation | loop fusion | flops 62720 | bytes 225792 | tf_op jit(solution)/shard_map/add | solution.py:769
Async XLA Ops:
  0.6 38.7 %copy-start = (bf16[49,16,16]{0,2,1:T(8,128)(2,1)S(1)}, bf16[49,16,16]{0,2,1:T(8,128)(2,1)}, u32[]{:S(2)}) copy-start(bf16[49,16,16]{0,2,1:T(8,128)(2,1)} %param.11) | copy-start | bytes 75268
  0.6 38.7 %copy-start.1 = (bf16[49,16,16]{0,2,1:T(8,128)(2,1)S(1)}, bf16[49,16,16]{0,2,1:T(8,128)(2,1)}, u32[]{:S(2)}) copy-start(bf16[49,16,16]{0,2,1:T(8,128)(2,1)} %param.12) | copy-start | bytes 75268

commit v5 on v4

--- a/solution.py
+++ b/solution.py
@@ -437,18 +437,6 @@
         return carry
 
     lax.fori_loop(0, 4, pair_in, 0)
-    for copy, cond in sends:
-        if cond is None:
-            copy.wait_send()
-        else:
-            pl.when(cond)(lambda copy=copy: copy.wait_send())
-
-    @pl.when(end)
-    def _():
-        for n, who in enumerate((mirror, ch)):
-            for j, off in enumerate((2, 1, 3)):
-                end_copy(n * 3 + j, who, peer(off)).wait_send()
-
     w0 = jnp.concatenate([w0_ref[:, lev].reshape(112, 128) for lev in range(7)], 1)
     y0 = dot(w0, rot[0:896, :])
     ys[0:7] = y0.reshape(7, 16, EDGES)
@@ -544,7 +532,8 @@
         who = ((zh + 1 - half) % 2) * 4 + lax.rem(xi + off, 4)
         return end_part(i, who, peer(off))
 
-    def pair_out(i, carry):
+    def pair_out(step, carry):
+        i = lax.rem(step + jnp.where(d == doms - 1, 2, 0), 4)
         both = [group_of(2 * i + n) for n in range(2)]
 
         def read(n, pos):
@@ -600,11 +589,13 @@
         pl.when(has_down)(lambda: to_up(who).wait_recv())
         return accum[who] + from_above[who].astype(F32) + from_below[who].astype(F32)
 
-    for half in range(2):
+    def along_x(half):
         for j in range(3):
             x_out[half * 3 + j] = finish(half * 4 + j).astype(BF16)
             to_peer(half * 3 + j, offs[j]).start()
         red[half] = finish(half * 4 + 3)
+
+    along_x(0)
 
     def gathered(half):
         total = red[half]
@@ -615,7 +606,7 @@
 
     @pl.when(end)
     def _():
-        for half in range(2):
+        for half in (1, 0):
             who = ((zh + 1 - half) % 2) * 4 + xi
             total = ghost_out[end_side, who].astype(F32)
             for j in range(3):
@@ -627,6 +618,7 @@
     z_out[...] = gathered(0).astype(BF16)
     across_z = rcopy(z_out, z_in, zs_send.at[0], zs_recv.at[0], other)
     across_z.start()
+    along_x(1)
 
     def read_z(n, pos):
         value = ys[pos] * factor
@@ -659,6 +651,17 @@
             end_peer(i).wait_send()
         end_home(0).wait_send()
         end_home(1).wait_send()
+    for copy, cond in sends:
+        if cond is None:
+            copy.wait_send()
+        else:
+            pl.when(cond)(lambda copy=copy: copy.wait_send())
+
+    @pl.when(end)
+    def _():
+        for n, who in enumerate((mirror, ch)):
+            for j, off in enumerate((2, 1, 3)):
+                end_copy(n * 3 + j, who, peer(off)).wait_send()
     across_z.wait_send()
     across_z.wait_recv()
     grad = red[1] + z_in[...].astype(F32)

time: 40.2 us -> 40.1 us (level)
  the two profiles are of different devices: /device:TPU:2 before, /device:TPU:1 now
where the time goes in v5:
time: 40.1 us; the launch traced here: 39.9 us
  Pallas kernels  38.5 us (96%)
  other arithmetic  0.7 us (2%)
  between operations  0.67 us (2%)
    pallas_call x1, Pallas kernels, on_device(): pl.pallas_call(body, out_shape=(jax.ShapeDtypeStruct((16, 16, K), F32), j...  38.5 us

profile of v5, /device:TPU:1, one launch (start us, length us, event | category | flops | bytes accessed | tf_op | source)
XLA Modules:
  0.0 39.9 jit_solution(4417034727811344401)
XLA Ops:
  0.6 0.0 copy-start
  0.6 0.0 copy-start.1
  0.7 38.5 %layer.1 = (f32[16,16,49]{2,1,0:T(8,128)S(1)}, f32[16,16,49]{2,1,0:T(8,128)S(1)}) custom-call(bf16[16,16,49]{2,1,0:T(8,128)(2,1)} %bitcast.12, bf16[16,16,49]{2,1,0:T(8,128)(2,1)} %bitcast.13, s32[8,16]{1,0:T(8,128)} %src_hbm.1, s32[8,16]{1,0:T(8,128)} %turn_hbm.1, s32[16]{0:T(128)} %cnt_hbm.1, s32[16]{0:T(128)} %slot_hbm.1, f32[455,256]{1,0:T(8,128)} %wig_hbm.1, ...), custom_call_target="tpu_custom_call" | custom-call | tf_op jit(solution)/shard_map/layer/pallas_call | solution.py:688
  39.2 0.0 copy-done
  39.2 0.0 copy-done.1
  39.2 0.7 %bitcast_add_fusion = (f32[49,16,16]{0,2,1:T(8,128)}, bf16[49,16,16]{0,2,1:T(8,128)(2,1)}) fusion(f32[16,16,49]{2,1,0:T(8,128)S(1)} %get-tuple-element.5, bf16[49,16,16]{0,2,1:T(8,128)(2,1)S(1)} %copy-done.1, f32[16,16,49]{2,1,0:T(8,128)S(1)} %get-tuple-element.4, bf16[49,16,16]{0,2,1:T(8,128)(2,1)S(1)} %copy-done), kind=kLoop, calls=%fused_computation | loop fusion | flops 62720 | bytes 225792 | tf_op jit(solution)/shard_map/add | solution.py:772
Async XLA Ops:
  0.6 38.6 %copy-start = (bf16[49,16,16]{0,2,1:T(8,128)(2,1)S(1)}, bf16[49,16,16]{0,2,1:T(8,128)(2,1)}, u32[]{:S(2)}) copy-start(bf16[49,16,16]{0,2,1:T(8,128)(2,1)} %param.11) | copy-start | bytes 75268
  0.6 38.6 %copy-start.1 = (bf16[49,16,16]{0,2,1:T(8,128)(2,1)S(1)}, bf16[49,16,16]{0,2,1:T(8,128)(2,1)}, u32[]{:S(2)}) copy-start(bf16[49,16,16]{0,2,1:T(8,128)(2,1)} %param.12) | copy-start | bytes 75268

commit v6 on v5

--- a/solution.py
+++ b/solution.py
@@ -604,6 +604,9 @@
             total = total + x_in[half * 3 + j].astype(F32)
         return total
 
+    z_out[...] = gathered(0).astype(BF16)
+    across_z = rcopy(z_out, z_in, zs_send.at[0], zs_recv.at[0], other)
+    across_z.start()
     @pl.when(end)
     def _():
         for half in (1, 0):
@@ -615,9 +618,6 @@
             end_sum[half] = total.astype(BF16)
             end_home(half).start()
 
-    z_out[...] = gathered(0).astype(BF16)
-    across_z = rcopy(z_out, z_in, zs_send.at[0], zs_recv.at[0], other)
-    across_z.start()
     along_x(1)
 
     def read_z(n, pos):

time: 40.1 us -> 40.1 us (level)
  no operation moved by 1% of the time
where the time goes in v6:
time: 40.1 us; the launch traced here: 39.9 us
  Pallas kernels  38.5 us (96%)
  other arithmetic  0.7 us (2%)
  between operations  0.67 us (2%)
    pallas_call x1, Pallas kernels, on_device(): pl.pallas_call(body, out_shape=(jax.ShapeDtypeStruct((16, 16, K), F32), j...  38.5 us

profile of v6, /device:TPU:1, one launch (start us, length us, event | category | flops | bytes accessed | tf_op | source)
XLA Modules:
  0.0 39.9 jit_solution(2476155238845652054)
XLA Ops:
  0.6 0.0 copy-start
  0.6 0.0 copy-start.1
  0.7 38.5 %layer.1 = (f32[16,16,49]{2,1,0:T(8,128)S(1)}, f32[16,16,49]{2,1,0:T(8,128)S(1)}) custom-call(bf16[16,16,49]{2,1,0:T(8,128)(2,1)} %bitcast.12, bf16[16,16,49]{2,1,0:T(8,128)(2,1)} %bitcast.13, s32[8,16]{1,0:T(8,128)} %src_hbm.1, s32[8,16]{1,0:T(8,128)} %turn_hbm.1, s32[16]{0:T(128)} %cnt_hbm.1, s32[16]{0:T(128)} %slot_hbm.1, f32[455,256]{1,0:T(8,128)} %wig_hbm.1, ...), custom_call_target="tpu_custom_call" | custom-call | tf_op jit(solution)/shard_map/layer/pallas_call | solution.py:688
  39.2 0.0 copy-done
  39.2 0.0 copy-done.1
  39.2 0.7 %bitcast_add_fusion = (f32[49,16,16]{0,2,1:T(8,128)}, bf16[49,16,16]{0,2,1:T(8,128)(2,1)}) fusion(f32[16,16,49]{2,1,0:T(8,128)S(1)} %get-tuple-element.5, bf16[49,16,16]{0,2,1:T(8,128)(2,1)S(1)} %copy-done.1, f32[16,16,49]{2,1,0:T(8,128)S(1)} %get-tuple-element.4, bf16[49,16,16]{0,2,1:T(8,128)(2,1)S(1)} %copy-done), kind=kLoop, calls=%fused_computation | loop fusion | flops 62720 | bytes 225792 | tf_op jit(solution)/shard_map/add | solution.py:772
Async XLA Ops:
  0.6 38.6 %copy-start = (bf16[49,16,16]{0,2,1:T(8,128)(2,1)S(1)}, bf16[49,16,16]{0,2,1:T(8,128)(2,1)}, u32[]{:S(2)}) copy-start(bf16[49,16,16]{0,2,1:T(8,128)(2,1)} %param.11) | copy-start | bytes 75268
  0.6 38.6 %copy-start.1 = (bf16[49,16,16]{0,2,1:T(8,128)(2,1)S(1)}, bf16[49,16,16]{0,2,1:T(8,128)(2,1)}, u32[]{:S(2)}) copy-start(bf16[49,16,16]{0,2,1:T(8,128)(2,1)} %param.12) | copy-start | bytes 75268
